TPU v7x, 32 devices: a whole 2x2x4 slice. The times are simulated.
32 devices in a mesh: fsdp: 16 (over z, y, x), tp: 2 (over core).
Axes of the slice: x: 2, y: 2, z: 4, core: 2. Of those that a mesh axis runs over, the one named last changes fastest.
Arguments:
- inputs: bfloat16 [4096, 4096], P('fsdp'), may hold values from -6 to 6
- value_grad: bfloat16 [4096, 1024], P('fsdp', 'tp'), may hold values from -24 to 24
- value_weight: bfloat16 [4096, 1024], P('tp', 'fsdp'), may hold values from -0.09375 to 0.09375
- counts: int32 [16, 4], P('fsdp'), may hold values from 1 to 232, as said below
- offsets: int32 [16, 4], P('fsdp'), may hold values from 0 to 248, as said below
Outputs:
- input_grad: bfloat16 [4096, 4096], P('fsdp', 'tp')
- weight_grad: float32 [4096, 1024], P('fsdp', 'tp')
Inputs may be any that keep to these rules, and one draw needn't show every extreme that they name: `offsets`: on each index of fsdp the 4 samples lie in order; each starts at a multiple of 8, at or after the 8-row-aligned end of the previous one, and all lie within the 256 rows; on some index the aligned blocks of its samples fill all 256 rows. `counts`: how many rows the samples of a row group fill varies widely between indices of fsdp.
All inputs are finite; a program needn't handle non-finite values.
Results may differ from a plain program's by a relative error of at most 0.0046.
Values may be sent and summed in bfloat16 or wider, within the bound.
A program may use at most 64 MiB of HBM per device.

v0:
```python
import math

import jax
import jax.numpy as jnp
from jax import lax
from jax.sharding import PartitionSpec as P


def local(inputs, value_grad, value_weight, counts, offsets):
    tok_rows = inputs.shape[0]
    row_block = min(128, tok_rows)
    positions = jnp.arange(tok_rows, dtype=jnp.int32)[:, None]
    starts = offsets[0][None, :]
    lengths = counts[0][None, :]
    inside = (positions >= starts) & (positions < starts + lengths)
    inverse_root = lax.rsqrt(lengths.astype(jnp.float32))
    row_factor = jnp.sum(jnp.where(inside, inverse_root, jnp.zeros_like(inverse_root)), axis=1)
    scaled = (value_grad.astype(jnp.float32) * row_factor[:, None]).astype(jnp.bfloat16)
    live_end = jnp.max(offsets[0] + counts[0])
    live_blocks = (live_end + row_block - 1) // row_block
    scaled_all = lax.all_gather(scaled, "tp", axis=1, tiled=True)
    empty_inputs = jnp.zeros((tok_rows, value_weight.shape[0]), jnp.float32)
    piece = lax.all_gather(value_weight, "fsdp", axis=1, tiled=True)

    def add_add_block(block_index, partial_value):
        lower = lax.dynamic_slice_in_dim(scaled_all, block_index * row_block, row_block, 0)
        before = lax.dynamic_slice_in_dim(partial_value, block_index * row_block, row_block, 0)
        product = lax.dot_general(
            lower, piece, (((1,), (1,)), ((), ())), preferred_element_type=jnp.float32
        )
        return lax.dynamic_update_slice_in_dim(
            partial_value, before + product, block_index * row_block, 0
        )

    result = lax.fori_loop(0, live_blocks, add_add_block, empty_inputs)
    input_grad = result.astype(jnp.bfloat16)
    normalizer = 1.0 / math.sqrt(counts.shape[1] * lax.axis_size("fsdp"))
    empty = jnp.zeros((inputs.shape[1], scaled.shape[1]), jnp.float32)

    def weight_add_block(block_index, partial_value):
        feature_rows = lax.dynamic_slice_in_dim(inputs, block_index * row_block, row_block, 0)
        grad_rows = lax.dynamic_slice_in_dim(scaled, block_index * row_block, row_block, 0)
        return partial_value + lax.dot_general(
            feature_rows, grad_rows, (((0,), (0,)), ((), ())), preferred_element_type=jnp.float32
        )

    result = lax.fori_loop(0, live_blocks, weight_add_block, empty)
    summed = lax.psum_scatter(result, "fsdp", scatter_dimension=0, tiled=True)
    return (input_grad, summed * normalizer)


def solution(mesh):
    in_specs = (P("fsdp", None), P("fsdp", "tp"), P("tp", "fsdp"), P("fsdp", None), P("fsdp", None))
    out_specs = (P("fsdp", "tp"), P("fsdp", "tp"))
    return jax.shard_map(local, mesh=mesh, in_specs=in_specs, out_specs=out_specs, check_vma=False)
```

profile of v0, /device:TPU:0, one launch (start us, length us, event | category | flops | bytes accessed | tf_op | source)
XLA Modules:
  0.0 276.6 jit_solution(10683928178615963049)
XLA Ops:
  7.2 0.0 all-gather.2.cloned.1.call-start
  7.2 0.7 all-gather.2.cloned.1.call-update
  7.9 0.0 reduce-scatter.2.cloned.1.call-start
  7.9 1.3 fusion.7
  9.9 0.7 rsqrt_bitcast_fusion
  10.6 0.7 add_bitcast_fusion
  11.3 0.7 select_reduce_fusion
  12.0 1.1 multiply_convert_fusion
  13.1 0.0 copy-start
  13.1 4.3 %broadcast_in_dim.30 = f32[4096,512]{1,0:T(8,128)} broadcast(f32[]{:T(128)} %constant.38.clone.1), dimensions={} | broadcast | bytes 8388612 | tf_op jit(solution)/shard_map/broadcast_in_dim | solution.py:38
  17.4 0.0 copy-done
  17.4 7.9 %while.21 = (s32[]{:T(128)}, f32[4096,512]{1,0:T(8,128)}, s32[]{:T(128)}, bf16[256,4096]{1,0:T(8,128)(2,1)S(1)}, bf16[256,512]{1,0:T(8,128)(2,1)S(1)}, /*index=5*/s32[]{:T(128)}, s32[]{:T(128)}, s32[]{:T(128)}, s32[]{:T(128)}) while((s32[]{:T(128)}, f32[4096,512]{1,0:T(8,128)}, s32[]{:T(128)}, bf16[256,4096]{1,0:T(8,128)(2,1)S(1)}, ...), condition=%wide.region_5.6_spmd, body=%wide.region_4.5_spmd.sunk | while | flops 538968064 | bytes 17958028 | solution.py:47
  17.4 7.9 %convolution_add_fusion.3 = f32[4096,512]{1,0:T(8,128)} fusion(f32[4096,512]{1,0:T(8,128)} %get-tuple-element.191, bf16[256,4096]{1,0:T(8,128)(2,1)S(1)} %get-tuple-element.202, s32[]{:T(128)S(6)} %select_n.24, bf16[256,512]{1,0:T(8,128)(2,1)S(1)} %get-tuple-element.203), kind=kOutput, calls=%fused_computation.4.clone.1 | convolution fusion | flops 538968064 | bytes 17957888 | tf_op jit(solution)/shard_map/while/body/dot_general | solution.py:43
  25.3 0.0 reduce-scatter.2.cloned.1.call-update
  25.3 2.3 all_gather.6
  27.6 61.5 %all-gather.2.cloned.1.call-done = bf16[2048,1024]{0,1:T(8,128)(2,1)} async-done(((bf16[2048,64]{0,1:T(8,128)(2,1)}), bf16[2048,1024]{0,1:T(8,128)(2,1)}) %all-gather.2.cloned.1.call-update) | async-done | bytes 4194320 | tf_op jit(solution)/shard_map/all_gather | solution.py:23
  89.1 6.4 %copy.9 = bf16[2048,1024]{1,0:T(8,128)(2,1)} copy(bf16[2048,1024]{0,1:T(8,128)(2,1)} %all-gather.2.cloned.1.call-done) | data formatting | bytes 8388608 | tf_op jit(solution)/shard_map/while | solution.py:35
  95.5 0.2 broadcast_in_dim.26
  95.7 3.8 %while.20 = (s32[]{:T(128)}, f32[256,2048]{1,0:T(8,128)S(1)}, s32[]{:T(128)}, bf16[256,1024]{1,0:T(8,128)(2,1)S(1)}, bf16[2048,1024]{1,0:T(8,128)(2,1)}, /*index=5*/s32[]{:T(128)}, s32[]{:T(128)}, s32[]{:T(128)}, s32[]{:T(128)}) while((s32[]{:T(128)}, f32[256,2048]{1,0:T(8,128)S(1)}, s32[]{:T(128)}, bf16[256,1024]{1,0:T(8,128)(2,1)S(1)}, ...), condition=%wide.region_3.4_spmd, body=%wide.region_2.3_spmd.sunk | while | flops 537133056 | bytes 6554763 | solution.py:35
  95.8 3.8 %fusion.16 = f32[256,2048]{1,0:T(8,128)S(1)} fusion(f32[256,2048]{1,0:T(8,128)S(1)} %get-tuple-element.164, s32[]{:T(128)S(6)} %select_n.23, bf16[2048,1024]{1,0:T(8,128)(2,1)} %get-tuple-element.176, bf16[256,1024]{1,0:T(8,128)(2,1)S(1)} %get-tuple-element.175), kind=kOutput, calls=%fused_computation.1.clone.1 | convolution fusion | flops 537133056 | bytes 6554624 | tf_op jit(solution)/shard_map/while/body/dot_general | solution.py:28
  99.6 1.1 convert_element_type.15
  100.7 167.2 %reduce-scatter.2.cloned.1.call-done = f32[256,512]{1,0:T(8,128)} async-done(((f32[4096,512]{1,0:T(8,128)}), f32[256,512]{1,0:T(8,128)}) %reduce-scatter.2.cloned.1.call-update) | async-done | bytes 524304 | tf_op jit(solution)/shard_map/reduce_scatter | solution.py:48
  267.9 1.9 broadcast_multiply_fusion
Async XLA Ops:
  7.2 81.9 %all-gather.2.cloned.1.call-start = ((), (), s32[]{:S(2)}) async-start(), calls=%async_computation.1 | async-start | bytes 4456448 | tf_op jit(solution)/shard_map/all_gather | solution.py:23
  7.9 260.0 %reduce-scatter.2.cloned.1.call-start = ((), (), s32[]{:S(2)}) async-start(), calls=%async_computation.2 | async-start | bytes 8912896 | tf_op jit(solution)/shard_map/reduce_scatter | solution.py:48
  13.1 4.3 %copy-start = (bf16[256,4096]{1,0:T(8,128)(2,1)S(1)}, bf16[256,4096]{1,0:T(8,128)(2,1)}, u32[]{:S(2)}) copy-start(bf16[256,4096]{1,0:T(8,128)(2,1)} %param.9) | copy-start | bytes 6291460
Sparse Core Ops, SparseCore 0:
  10.7 78.3 all-gather.1
  91.4 176.4 reduce-scatter.1
where the time goes:
time: 279 us; the launch traced here: 277 us
  waiting for transfers between devices  229 us (82%)
  between operations  14.7 us (5%)
  matrix products  11.7 us (4%)
  local copies, waits for them, and re-layouts  10.9 us (4%)
  other arithmetic  7.43 us (3%)
    reduce_scatter x1, waiting for transfers between devices, local(): summed = lax.psum_scatter(result, 'fsdp', scatter_dimension=0, tiled=True)  167 us
    all_gather x1, waiting for transfers between devices, local(): piece = lax.all_gather(value_weight, 'fsdp', axis=1, tiled=True)  61.5 us
    dot_general x1, matrix products, weight_add_block(): lax.dot_general(feature_rows, grad_rows, (((0,), (0,)), ((), ())), prefer...  7.88 us
    while x1, local copies, waits for them, and re-layouts, local(): result = lax.fori_loop(0, live_blocks, add_add_block, empty_inputs)  6.42 us
  transfers between devices with their start and end apart: 2, of which 2 were waited for; matrix products, arithmetic and copies ran while one was open for 10% of the time, Pallas kernels for 0%

commit v1 on v0

--- a/solution.py
+++ b/solution.py
@@ -1,21 +1,32 @@
+import functools
 import math
 
 import jax
 import jax.numpy as jnp
 from jax import lax
+from jax.experimental import pallas as pl
+from jax.experimental.pallas import tpu as pltpu
 from jax.sharding import PartitionSpec as P
 
-
-def local(inputs, value_grad, value_weight, counts, offsets):
-    tok_rows = inputs.shape[0]
-    row_block = min(128, tok_rows)
-    positions = jnp.arange(tok_rows, dtype=jnp.int32)[:, None]
+MESH = pl.DeviceIdType.MESH
+GROUP = 4
+VMEM_ROOM = 48 * 2**20
+
+
+def scale_rows(value_grad, counts, offsets):
+    positions = jnp.arange(value_grad.shape[0], dtype=jnp.int32)[:, None]
     starts = offsets[0][None, :]
     lengths = counts[0][None, :]
     inside = (positions >= starts) & (positions < starts + lengths)
     inverse_root = lax.rsqrt(lengths.astype(jnp.float32))
     row_factor = jnp.sum(jnp.where(inside, inverse_root, jnp.zeros_like(inverse_root)), axis=1)
-    scaled = (value_grad.astype(jnp.float32) * row_factor[:, None]).astype(jnp.bfloat16)
+    return (value_grad.astype(jnp.float32) * row_factor[:, None]).astype(jnp.bfloat16)
+
+
+def general(inputs, value_grad, value_weight, counts, offsets):
+    tok_rows = inputs.shape[0]
+    row_block = min(128, tok_rows)
+    scaled = scale_rows(value_grad, counts, offsets)
     live_end = jnp.max(offsets[0] + counts[0])
     live_blocks = (live_end + row_block - 1) // row_block
     scaled_all = lax.all_gather(scaled, "tp", axis=1, tiled=True)
@@ -49,7 +60,236 @@
     return (input_grad, summed * normalizer)
 
 
+def kernel(
+    n, normalizer, x_ref, s_ref, wt_ref, dx_ref, dw_ref,
+    s_own, s_sib, x_all, w_all, part_out, part_in, dx_out, dx_in,
+    w_send, w_recv, s_send, s_recv, c_send, c_recv, x_send, x_recv,
+    g_send, g_recv, p_send, p_recv, o_send, o_recv,
+):
+    nz = n // GROUP
+    me = lax.axis_index("fsdp")
+    core = lax.axis_index("tp")
+    sib = 1 - core
+    z = me // GROUP
+    quarter = me % GROUP
+    dx = 1 - 2 * (me % 2)
+    dy = 2 - 4 * ((me // 2) % 2)
+    steps = (0, dx, dy, dx + dy)
+    tok = s_ref.shape[0]
+    half = s_ref.shape[1]
+    wcols = wt_ref.shape[0]
+    fq = w_all.shape[1]
+    zrows = GROUP * wcols
+    hr = x_all.shape[2]
+    order = [k for k in range(nz // 2, nz)] + [k for k in range(1, nz // 2)] + [0]
+
+    def remote(src, dst, send, recv, dev):
+        return pltpu.make_async_remote_copy(
+            src_ref=src, dst_ref=dst, send_sem=send, recv_sem=recv,
+            device_id=dev, device_id_type=MESH,
+        )
+
+    barrier = pltpu.get_barrier_semaphore()
+    targets = [(me + steps[j], core) for j in range(1, GROUP)] + [(me, sib)]
+    for k in range(1, nz):
+        other = ((z + k) % nz) * GROUP + quarter
+        targets += [(other, core), (other, sib)]
+    for dev in targets:
+        pl.semaphore_signal(barrier, inc=1, device_id=dev, device_id_type=MESH)
+    pl.semaphore_wait(barrier, len(targets))
+
+    def w_rows(f):
+        return pl.ds(pl.multiple_of(f * wcols, wcols), wcols)
+
+    def lanes(start, size):
+        return pl.ds(pl.multiple_of(start, 128), size)
+
+    def slot(j):
+        return pl.ds(j * tok, tok)
+
+    w_copies, s_copies, x_copies = {}, {}, {}
+    for j in range(1, GROUP):
+        w_copies[j] = remote(
+            wt_ref.at[:, lanes((quarter + steps[j]) * fq, fq)], w_all.at[w_rows(me), :],
+            w_send.at[j], w_recv.at[j], (me + steps[j], core))
+        w_copies[j].start()
+    own_copy = remote(s_ref, s_sib.at[slot(0), :], c_send.at[0], c_recv.at[0], (me, sib))
+    own_copy.start()
+    for j in (3, 1, 2):
+        s_copies[j] = remote(
+            s_ref, s_own.at[slot(j), :], s_send.at[j], s_recv.at[j], (me + steps[j], core))
+        s_copies[j].start()
+
+    def x_lanes(k, q):
+        zk = (z + k) % nz
+        return lanes(((zk * GROUP + q) * 2 + core) * hr, hr)
+
+    for k in order:
+        for j in (3, 1, 2):
+            x_copies[k, j] = remote(
+                x_ref.at[:, x_lanes(k, quarter + steps[j])], x_all.at[k, slot(j), :],
+                x_send.at[k, j], x_recv.at[k, j], (me + steps[j], core))
+            x_copies[k, j].start()
+    w_all[w_rows(me), :] = wt_ref[:, lanes(quarter * fq, fq)]
+    s_own[slot(0), :] = s_ref[...]
+    for k in range(nz):
+        x_all[k, slot(0), :] = x_ref[:, x_lanes(k, quarter)]
+
+    def chain(origin, way, k):
+        rows = pl.ds(pl.multiple_of(origin * zrows, zrows), zrows)
+        dev = (me + GROUP * way, core)
+        return remote(w_all.at[rows, :], w_all.at[rows, :],
+                      g_send.at[(1 - way) // 2, k], g_recv.at[origin], dev)
+
+    def chain_step(k):
+        for way in (1, -1):
+            origin = z - way * k
+            here = (origin >= 0) & (origin < nz)
+            onward = here & (z + way >= 0) & (z + way < nz)
+            if k > 0:
+                @pl.when(here)
+                def _():
+                    chain(origin, -way, k).wait_recv()
+
+            @pl.when(onward)
+            def _():
+                chain(origin, way, k).start()
+
+    for j in range(1, GROUP):
+        w_copies[j].wait_recv()
+    chain_step(0)
+
+    core_copies = [own_copy]
+    for j in (1, 2, 3):
+        s_copies[j].wait_recv()
+        copy = remote(s_own.at[slot(j), :], s_sib.at[slot(j), :], c_send.at[j], c_recv.at[j], (me, sib))
+        copy.start()
+        core_copies.append(copy)
+    if nz > 1:
+        chain_step(1)
+    for copy in core_copies:
+        copy.wait_recv()
+
+    p_copies = []
+    own_part = None
+    next_step = 2
+    for k in order:
+        for j in range(1, GROUP):
+            x_copies[k, j].wait_recv()
+        feature_rows = x_all[k]
+        dims = (((0,), (0,)), ((), ()))
+        for side, grads, dst_core in ((0, s_own, core), (1, s_sib, sib)):
+            part = lax.dot_general(feature_rows, grads[...], dims, preferred_element_type=jnp.float32)
+            if k == 0 and side == 0:
+                own_part = part
+                dw_ref[pl.ds(pl.multiple_of(core * hr, hr), hr), :] = part
+                continue
+            part_out[k, side] = part.astype(jnp.bfloat16)
+            dev = (((z + k) % nz) * GROUP + quarter, dst_core)
+            copy = remote(part_out.at[k, side], part_in.at[k, side], p_send.at[k, side], p_recv.at[k, side], dev)
+            copy.start()
+            p_copies.append(copy)
+        if next_step < nz:
+            chain_step(next_step)
+            next_step += 1
+
+    o_copies = {}
+    own_rows = pl.ds(pl.multiple_of(core * half, half), half)
+    sib_rows = pl.ds(pl.multiple_of(sib * half, half), half)
+    for j in (3, 1, 2, 0):
+        product = jnp.dot(s_own[slot(j), :], w_all[own_rows, :], preferred_element_type=jnp.float32)
+        product += jnp.dot(s_sib[slot(j), :], w_all[sib_rows, :], preferred_element_type=jnp.float32)
+        if j == 0:
+            dx_ref[:, lanes(quarter * fq, fq)] = product.astype(jnp.bfloat16)
+        else:
+            dx_out[j] = product.astype(jnp.bfloat16)
+            o_copies[j] = remote(dx_out.at[j], dx_in.at[j], o_send.at[j], o_recv.at[j], (me + steps[j], core))
+            o_copies[j].start()
+
+    for copy in p_copies:
+        copy.wait_recv()
+    own_half = pl.ds(pl.multiple_of(core * hr, hr), hr)
+    sib_half = pl.ds(pl.multiple_of(sib * hr, hr), hr)
+    total = dw_ref[own_half, :]
+    for k in range(1, nz):
+        total += part_in[k, 0].astype(jnp.float32)
+    dw_ref[own_half, :] = total * normalizer
+    total = part_in[0, 1].astype(jnp.float32)
+    for k in range(1, nz):
+        total += part_in[k, 1].astype(jnp.float32)
+    dw_ref[sib_half, :] = total * normalizer
+
+    for j in (1, 2, 3):
+        o_copies[j].wait_recv()
+        dx_ref[:, lanes((quarter + steps[j]) * fq, fq)] = dx_in[j]
+
+    for group in (w_copies, s_copies, x_copies, o_copies):
+        for copy in group.values():
+            copy.wait_send()
+    for copy in core_copies + p_copies:
+        copy.wait_send()
+    for k in range(nz):
+        for way in (1, -1):
+            origin = z - way * k
+
+            @pl.when((origin >= 0) & (origin < nz) & (z + way >= 0) & (z + way < nz))
+            def _():
+                chain(origin, way, k).wait_send()
+
+
+def fused(n, inputs, value_grad, value_weight, counts, offsets):
+    tok, width = inputs.shape
+    half = value_grad.shape[1]
+    wfeat, wcols = value_weight.shape
+    nz = n // GROUP
+    fq = wfeat // GROUP
+    hr = width // n // 2
+    bf, dma = jnp.bfloat16, pltpu.SemaphoreType.DMA
+    normalizer = 1.0 / math.sqrt(counts.shape[1] * n)
+    scaled = scale_rows(value_grad, counts, offsets)
+    vmem = pl.BlockSpec(memory_space=pltpu.VMEM)
+    return pl.pallas_call(
+        functools.partial(kernel, n, normalizer),
+        out_shape=(
+            jax.ShapeDtypeStruct((tok, wfeat), bf),
+            jax.ShapeDtypeStruct((2 * hr, half), jnp.float32),
+        ),
+        in_specs=[vmem] * 3,
+        out_specs=(vmem, vmem),
+        scratch_shapes=[
+            pltpu.VMEM((GROUP * tok, half), bf),
+            pltpu.VMEM((GROUP * tok, half), bf),
+            pltpu.VMEM((nz, GROUP * tok, hr), bf),
+            pltpu.VMEM((n * wcols, fq), bf),
+            pltpu.VMEM((nz, 2, hr, half), bf),
+            pltpu.VMEM((nz, 2, hr, half), bf),
+            pltpu.VMEM((GROUP, tok, fq), bf),
+            pltpu.VMEM((GROUP, tok, fq), bf),
+            dma((GROUP,)), dma((GROUP,)),
+            dma((GROUP,)), dma((GROUP,)),
+            dma((GROUP,)), dma((GROUP,)),
+            dma((nz, GROUP)), dma((nz, GROUP)),
+            dma((2, nz)), dma((nz,)),
+            dma((nz, 2)), dma((nz, 2)),
+            dma((GROUP,)), dma((GROUP,)),
+        ],
+        compiler_params=pltpu.CompilerParams(
+            collective_id=0, has_side_effects=True, vmem_limit_bytes=VMEM_ROOM
+        ),
+    )(inputs, scaled, value_weight.T)
+
+
 def solution(mesh):
+    n, tp = mesh.shape["fsdp"], mesh.shape["tp"]
+
+    def local(inputs, value_grad, value_weight, counts, offsets):
+        hr = inputs.shape[1] // n // 2
+        fits = tp == 2 and n % GROUP == 0 and n > GROUP and hr % 128 == 0
+        fits = fits and value_weight.shape[1] % 16 == 0
+        if fits:
+            return fused(n, inputs, value_grad, value_weight, counts, offsets)
+        return general(inputs, value_grad, value_weight, counts, offsets)
+
     in_specs = (P("fsdp", None), P("fsdp", "tp"), P("tp", "fsdp"), P("fsdp", None), P("fsdp", None))
     out_specs = (P("fsdp", "tp"), P("fsdp", "tp"))
     return jax.shard_map(local, mesh=mesh, in_specs=in_specs, out_specs=out_specs, check_vma=False)

time: 279 us -> 64.9 us (0.23)
  waiting for transfers between devices: 229 us -> 0 us
  Pallas kernels: 0 us -> 56.5 us
  between operations: 14.7 us -> 0.66 us
  matrix products: 11.7 us -> 0 us
  local copies, waits for them, and re-layouts: 10.9 us -> 4.3 us
  other arithmetic: 7.43 us -> 3.13 us
    reduce_scatter x1 -> x0, waiting for transfers between devices: 167 us -> none  [local(): summed = lax.psum_scatter(result, 'fsdp', scatter_dimension=0, tiled=True)]
    all_gather x1 -> x0, waiting for transfers between devices: 61.5 us -> none  [local(): piece = lax.all_gather(value_weight, 'fsdp', axis=1, tiled=True)]
    pallas_call x0 -> x1, Pallas kernels: none -> 56.5 us  [fused(): pl.pallas_call(functools.partial(kernel, n, normalizer), out_shape=(jax.S...]
    dot_general x2 -> x0, matrix products: 11.7 us -> none  [the longest x1 7.88 us: weight_add_block(): lax.dot_general(feature_rows, grad_rows, (((0,), (0,)), ((), ())), prefer...]
    while x1 -> x0, local copies, waits for them, and re-layouts: 6.42 us -> none  [local(): result = lax.fori_loop(0, live_blocks, add_add_block, empty_inputs)]
    broadcast_in_dim x2 -> x0, local copies, waits for them, and re-layouts: 4.52 us -> none  [the longest x1 4.29 us: local(): empty = jnp.zeros((inputs.shape[1], scaled.shape[1]), jnp.float32)]
    unnamed x2 -> x6, local copies, waits for them, and re-layouts: 0.01 us -> 4.3 us
  transfers between devices with their start and end apart: 2 -> 0, of which waited for: 2 -> 0; matrix products, arithmetic and copies ran while one was open for 10% -> 0% of each run, Pallas kernels for 0% -> 0%
where the time goes in v1:
time: 64.9 us; the launch traced here: 64.6 us
  Pallas kernels  56.5 us (87%)
  local copies, waits for them, and re-layouts  4.3 us (7%)
  other arithmetic  3.13 us (5%)
  between operations  0.66 us (1%)
    pallas_call x1, Pallas kernels, fused(): pl.pallas_call(functools.partial(kernel, n, normalizer), out_shape=(jax.S...  56.5 us
    unnamed x6, local copies, waits for them, and re-layouts  4.3 us

profile of v1, /device:TPU:0, one launch (start us, length us, event | category | flops | bytes accessed | tf_op | source)
XLA Modules:
  0.0 64.6 jit_solution(6430463599787322031)
XLA Ops:
  0.6 0.7 %rsqrt_bitcast_fusion = f32[4]{0:T(128)S(1)} fusion(s32[1,4]{1,0:T(1,128)} %param.8), kind=kLoop, calls=%fused_computation.5 | loop fusion | flops 4 | bytes 32 | tf_op jit(solution)/shard_map/jit(_where)/broadcast_in_dim | solution.py:22
  1.3 0.7 %add_bitcast_fusion = s32[4]{0:T(128)S(1)} fusion(s32[1,4]{1,0:T(1,128)} %param.9, s32[1,4]{1,0:T(1,128)} %param.8), kind=kLoop, calls=%fused_computation.6 | loop fusion | flops 4 | bytes 48 | tf_op jit(solution)/shard_map/lt | solution.py:20
  2.0 0.7 %select_reduce_fusion = f32[256]{0:T(256)S(1)} fusion(f32[4]{0:T(128)S(1)} %rsqrt_bitcast_fusion, s32[4]{0:T(128)S(1)} %add_bitcast_fusion, s32[4]{0:T(128)} %bitcast.7), kind=kLoop, calls=%fused_computation.1 | loop fusion | flops 4864 | bytes 1072 | tf_op jit(solution)/shard_map/reduce_sum | solution.py:22
  2.7 1.1 %multiply_convert_fusion.s_ref = bf16[256,512]{1,0:T(8,128)(2,1)S(1)} fusion(bf16[256,512]{1,0:T(8,128)(2,1)} %param.6, f32[256]{0:T(256)S(1)} %select_reduce_fusion), kind=kLoop, calls=%fused_computation | loop fusion | flops 393216 | bytes 525312 | tf_op jit(solution)/shard_map/convert_element_type | solution.py:23
  3.8 0.0 copy-start
  3.8 1.6 %copy-done = bf16[256,4096]{1,0:T(8,128)(2,1)S(1)} copy-done((bf16[256,4096]{1,0:T(8,128)(2,1)S(1)}, bf16[256,4096]{1,0:T(8,128)(2,1)}, u32[]{:S(2)}) %copy-start) | copy-done | bytes 2097176
  5.4 0.0 copy-start.1
  5.4 0.9 %copy-done.1 = bf16[2048,64]{0,1:T(8,128)(2,1)S(1)} copy-done((bf16[2048,64]{0,1:T(8,128)(2,1)S(1)}, bf16[2048,64]{0,1:T(8,128)(2,1)}, u32[]{:S(2)}) %copy-start.1) | copy-done | bytes 262168
  6.3 56.5 %shard_map.68 = (bf16[256,2048]{1,0:T(8,128)(2,1)S(1)}, f32[256,512]{1,0:T(8,128)S(1)}) custom-call(bf16[256,4096]{1,0:T(8,128)(2,1)S(1)} %copy-done, bf16[256,512]{1,0:T(8,128)(2,1)S(1)} %multiply_convert_fusion.s_ref, bf16[64,2048]{1,0:T(8,128)(2,1)S(1)} %bitcast.6), custom_call_target="tpu_custom_call" | custom-call | tf_op jit(solution)/shard_map/pallas_call | solution.py:251
  62.9 1.0 %copy.9 = bf16[256,2048]{1,0:T(8,128)(2,1)} copy(bf16[256,2048]{1,0:T(8,128)(2,1)S(1)} %get-tuple-element.4) | data formatting | bytes 2097152
  63.8 0.8 %copy.10 = f32[256,512]{1,0:T(8,128)} copy(f32[256,512]{1,0:T(8,128)S(1)} %get-tuple-element.5) | data formatting | bytes 1048576
Async XLA Ops:
  3.8 1.6 %copy-start = (bf16[256,4096]{1,0:T(8,128)(2,1)S(1)}, bf16[256,4096]{1,0:T(8,128)(2,1)}, u32[]{:S(2)}) copy-start(bf16[256,4096]{1,0:T(8,128)(2,1)} %x_ref.1) | copy-start | bytes 6291460
  5.4 0.9 %copy-start.1 = (bf16[2048,64]{0,1:T(8,128)(2,1)S(1)}, bf16[2048,64]{0,1:T(8,128)(2,1)}, u32[]{:S(2)}) copy-start(bf16[2048,64]{0,1:T(8,128)(2,1)} %param.7) | copy-start | bytes 786436

commit v2 on v1

v2 whole, which is shorter than its diff:
```python
import functools
import math

import jax
import jax.numpy as jnp
from jax import lax
from jax.experimental import pallas as pl
from jax.experimental.pallas import tpu as pltpu
from jax.sharding import PartitionSpec as P

MESH = pl.DeviceIdType.MESH
GROUP = 4
VMEM_ROOM = 48 * 2**20


def scale_rows(value_grad, counts, offsets):
    positions = jnp.arange(value_grad.shape[0], dtype=jnp.int32)[:, None]
    starts = offsets[0][None, :]
    lengths = counts[0][None, :]
    inside = (positions >= starts) & (positions < starts + lengths)
    inverse_root = lax.rsqrt(lengths.astype(jnp.float32))
    row_factor = jnp.sum(jnp.where(inside, inverse_root, jnp.zeros_like(inverse_root)), axis=1)
    return (value_grad.astype(jnp.float32) * row_factor[:, None]).astype(jnp.bfloat16)


def general(inputs, value_grad, value_weight, counts, offsets):
    tok_rows = inputs.shape[0]
    row_block = min(128, tok_rows)
    scaled = scale_rows(value_grad, counts, offsets)
    live_end = jnp.max(offsets[0] + counts[0])
    live_blocks = (live_end + row_block - 1) // row_block
    scaled_all = lax.all_gather(scaled, "tp", axis=1, tiled=True)
    empty_inputs = jnp.zeros((tok_rows, value_weight.shape[0]), jnp.float32)
    piece = lax.all_gather(value_weight, "fsdp", axis=1, tiled=True)

    def add_add_block(block_index, partial_value):
        lower = lax.dynamic_slice_in_dim(scaled_all, block_index * row_block, row_block, 0)
        before = lax.dynamic_slice_in_dim(partial_value, block_index * row_block, row_block, 0)
        product = lax.dot_general(
            lower, piece, (((1,), (1,)), ((), ())), preferred_element_type=jnp.float32
        )
        return lax.dynamic_update_slice_in_dim(
            partial_value, before + product, block_index * row_block, 0
        )

    result = lax.fori_loop(0, live_blocks, add_add_block, empty_inputs)
    input_grad = result.astype(jnp.bfloat16)
    normalizer = 1.0 / math.sqrt(counts.shape[1] * lax.axis_size("fsdp"))
    empty = jnp.zeros((inputs.shape[1], scaled.shape[1]), jnp.float32)

    def weight_add_block(block_index, partial_value):
        feature_rows = lax.dynamic_slice_in_dim(inputs, block_index * row_block, row_block, 0)
        grad_rows = lax.dynamic_slice_in_dim(scaled, block_index * row_block, row_block, 0)
        return partial_value + lax.dot_general(
            feature_rows, grad_rows, (((0,), (0,)), ((), ())), preferred_element_type=jnp.float32
        )

    result = lax.fori_loop(0, live_blocks, weight_add_block, empty)
    summed = lax.psum_scatter(result, "fsdp", scatter_dimension=0, tiled=True)
    return (input_grad, summed * normalizer)


def kernel(
    n, normalizer, counts_ref, offsets_ref, x_hbm, g_hbm, wt_hbm, dx_ref, dw_ref,
    x_ref, g_ref, wt_ref, s_ref, s_own, s_sib, x_all, w_all, part_own, part_out, part_in,
    swap_out, swap_in, dx_out, dx_in,
    local_sem, w_send, w_recv, s_send, s_recv, c_send, c_recv, x_send, x_recv,
    g_send, g_recv, p_send, p_recv, o_send, o_recv, swap_send, swap_recv,
):
    nz = n // GROUP
    me = lax.axis_index("fsdp")
    core = lax.axis_index("tp")
    sib = 1 - core
    z = me // GROUP
    quarter = me % GROUP
    dx = 1 - 2 * (me % 2)
    dy = 2 - 4 * ((me // 2) % 2)
    steps = (0, dx, dy, dx + dy)
    tok, half = s_ref.shape
    wcols = wt_ref.shape[0]
    fq = w_all.shape[1]
    zrows = GROUP * wcols
    hr = x_all.shape[2]
    upper = (2 * z) // nz
    order = [a + upper * (nz - 1 - 2 * a) for a in
             list(range(nz - 1, nz // 2 - 1, -1)) + list(range(nz // 2))]

    fetch_g = pltpu.make_async_copy(g_hbm, g_ref, local_sem.at[0])
    fetch_w = pltpu.make_async_copy(wt_hbm, wt_ref, local_sem.at[1])
    fetch_x = pltpu.make_async_copy(x_hbm, x_ref, local_sem.at[2])
    for fetch in (fetch_g, fetch_w, fetch_x):
        fetch.start()

    def remote(src, dst, send, recv, dev):
        return pltpu.make_async_remote_copy(
            src_ref=src, dst_ref=dst, send_sem=send, recv_sem=recv,
            device_id=dev, device_id_type=MESH,
        )

    barrier = pltpu.get_barrier_semaphore()
    for j in range(1, GROUP):
        pl.semaphore_signal(barrier, inc=1, device_id=(me + steps[j], core), device_id_type=MESH)
    pl.semaphore_signal(barrier, inc=1, device_id=(me, sib), device_id_type=MESH)
    ways = ((0, 1, z < nz - 1, z > 0), (1, -1, z > 0, z < nz - 1))
    for side, way, onward, behind in ways:
        @pl.when(onward)
        def _():
            pl.semaphore_signal(barrier, inc=1, device_id=(me + GROUP * way, core), device_id_type=MESH)

    fetch_g.wait()
    positions = lax.broadcasted_iota(jnp.int32, (tok, 128), 0)
    factor = jnp.zeros((tok, 128), jnp.float32)
    for i in range(counts_ref.shape[1]):
        start = jnp.full((tok, 128), offsets_ref[0, i], jnp.int32)
        length = jnp.full((tok, 128), counts_ref[0, i], jnp.int32)
        inside = (positions >= start) & (positions < start + length)
        factor += jnp.where(inside, lax.rsqrt(length.astype(jnp.float32)), 0.0)
    for i in range(half // 128):
        cols = slice(i * 128, (i + 1) * 128)
        scaled = (g_ref[:, cols].astype(jnp.float32) * factor).astype(jnp.bfloat16)
        s_ref[:, cols] = scaled
        s_own[0:tok, cols] = scaled
    fetch_w.wait()

    inner = (z > 0) & (z < nz - 1)

    @pl.when(inner)
    def _():
        pl.semaphore_wait(barrier, GROUP + 2)

    @pl.when(jnp.logical_not(inner))
    def _():
        pl.semaphore_wait(barrier, GROUP + 1)

    def w_rows(f):
        return pl.ds(pl.multiple_of(f * wcols, wcols), wcols)

    def lanes(start, size):
        return pl.ds(pl.multiple_of(start, 128), size)

    def slot(j):
        return pl.ds(j * tok, tok)

    w_copies, s_copies, x_copies = {}, {}, {}
    for j in (3, 1, 2):
        w_copies[j] = remote(
            wt_ref.at[:, lanes((quarter + steps[j]) * fq, fq)], w_all.at[w_rows(me), :],
            w_send.at[j], w_recv.at[j], (me + steps[j], core))
        w_copies[j].start()
    for j in (1, 2):
        s_copies[j] = remote(
            s_ref, s_own.at[slot(j), :], s_send.at[j], s_recv.at[j], (me + steps[j], core))
        s_copies[j].start()
    core_copies = [remote(s_ref, s_sib.at[slot(0), :], c_send.at[0], c_recv.at[0], (me, sib))]
    core_copies[0].start()
    fetch_x.wait()

    def x_lanes(i, q):
        return lanes(((order[i] * GROUP + q) * 2 + core) * hr, hr)

    def x_start(i):
        for j in (3, 1, 2):
            x_copies[i, j] = remote(
                x_ref.at[:, x_lanes(i, quarter + steps[j])], x_all.at[i, slot(j), :],
                x_send.at[i, j], x_recv.at[i, j], (me + steps[j], core))
            x_copies[i, j].start()

    x_start(0)
    w_all[w_rows(me), :] = wt_ref[:, lanes(quarter * fq, fq)]
    for i in range(nz):
        x_all[i, slot(0), :] = x_ref[:, x_lanes(i, quarter)]

    def chain(origin, way, k, h):
        rows = pl.ds(pl.multiple_of(origin * zrows + h * (zrows // 2), zrows // 2), zrows // 2)
        dev = (me + GROUP * way, core)
        return remote(w_all.at[rows, :], w_all.at[rows, :],
                      g_send.at[(1 - way) // 2, k, h], g_recv.at[origin, h], dev)

    def chain_step(k):
        for h in range(2):
            for side, way, onward, behind in ways:
                origin = z - way * k
                here = (origin >= 0) & (origin < nz)
                if k > 0:
                    @pl.when(here)
                    def _():
                        chain(origin, -way, k, h).wait_recv()

                @pl.when(here & onward)
                def _():
                    chain(origin, way, k, h).start()

    for j in range(1, GROUP):
        w_copies[j].wait_recv()
    chain_step(0)

    def to_core(j):
        copy = remote(s_own.at[slot(j), :], s_sib.at[slot(j), :], c_send.at[j], c_recv.at[j], (me, sib))
        copy.start()
        core_copies.append(copy)

    relays = []
    for j, onto in ((1, 2), (2, 1)):
        s_copies[j].wait_recv()
        first = (j - 1) * (tok // 2)
        copy = remote(
            s_own.at[pl.ds(j * tok + first, tok // 2), :],
            s_own.at[pl.ds(3 * tok + first, tok // 2), :],
            s_send.at[2 + j], s_recv.at[2 + j], (me + steps[onto], core))
        copy.start()
        relays.append(copy)
    for i in range(1, nz):
        x_start(i)
    for j in (1, 2):
        to_core(j)
    chain_step(1)
    for copy in relays:
        copy.wait_recv()
    to_core(3)
    for copy in core_copies:
        copy.wait_recv()

    def partial_copy(t, side, lane, way):
        return remote(part_out.at[t, lane], part_in.at[side, t, lane],
                      p_send.at[t, lane], p_recv.at[side, t, lane], (me + GROUP * way, core))

    def toward(t, side):
        return t > z if side == 0 else t < z

    def block(i):
        t = order[i]
        for j in range(1, GROUP):
            x_copies[i, j].wait_recv()
        feature_rows = x_all[i]
        dims = (((0,), (0,)), ((), ()))
        for lane, grads in ((1, s_sib), (0, s_own)):
            part = lax.dot_general(feature_rows, grads[...], dims, preferred_element_type=jnp.float32)
            part_own[t, lane] = part
            for side, way, onward, behind in ways:
                @pl.when(toward(t, side) & jnp.logical_not(behind))
                def _():
                    part_out[t, lane] = part_own[t, lane].astype(jnp.bfloat16)
                    partial_copy(t, side, lane, way).start()

    def forward(i):
        t = order[i]
        for lane in (1, 0):
            for side, way, onward, behind in ways:
                @pl.when(toward(t, side) & behind)
                def _():
                    copy = partial_copy(t, side, lane, way)
                    copy.wait_recv()
                    part_out[t, lane] = (
                        part_own[t, lane] + part_in[side, t, lane].astype(jnp.float32)
                    ).astype(jnp.bfloat16)
                    copy.start()

    block(0)
    for k in range(2, nz):
        chain_step(k)
        if k == 2:
            block(1)

    o_copies = {}
    own_rows = pl.ds(pl.multiple_of(core * half, half), half)
    sib_rows = pl.ds(pl.multiple_of(sib * half, half), half)
    for j in (3, 1, 2, 0):
        product = jnp.dot(s_own[slot(j), :], w_all[own_rows, :], preferred_element_type=jnp.float32)
        product += jnp.dot(s_sib[slot(j), :], w_all[sib_rows, :], preferred_element_type=jnp.float32)
        if j == 0:
            dx_ref[:, lanes(quarter * fq, fq)] = product.astype(jnp.bfloat16)
        else:
            dx_out[j] = product.astype(jnp.bfloat16)
            o_copies[j] = remote(dx_out.at[j], dx_in.at[j], o_send.at[j], o_recv.at[j], (me + steps[j], core))
            o_copies[j].start()

    started = 2 if nz > 2 else 1
    for i in range(nz - started):
        block(i + started)
        forward(i)
    for i in range(nz - started, nz):
        forward(i)

    swap = remote(swap_out, swap_in, swap_send, swap_recv, (me, sib))
    mine = pl.ds(pl.multiple_of(core * hr, hr), hr)
    for lane in (1, 0):
        for side, way, onward, behind in ways:
            @pl.when(behind)
            def _():
                partial_copy(z, side, lane, -way).wait_recv()
                part_own[z, lane] = part_own[z, lane] + part_in[side, z, lane].astype(jnp.float32)
        total = part_own[z, lane] * normalizer
        if lane == 1:
            swap_out[...] = total
            swap.start()
        else:
            dw_ref[mine, :] = total

    for j in (1, 2, 3):
        o_copies[j].wait_recv()
        dx_ref[:, lanes((quarter + steps[j]) * fq, fq)] = dx_in[j]
    swap.wait_recv()
    dw_ref[pl.ds(pl.multiple_of(sib * hr, hr), hr), :] = swap_in[...]

    for group in (w_copies, s_copies, x_copies, o_copies):
        for copy in group.values():
            copy.wait_send()
    for copy in core_copies + relays + [swap]:
        copy.wait_send()
    for t in range(nz):
        for lane in range(2):
            for side, way, onward, behind in ways:
                @pl.when(toward(t, side))
                def _():
                    partial_copy(t, side, lane, way).wait_send()
    for k in range(nz):
        for h in range(2):
            for side, way, onward, behind in ways:
                origin = z - way * k

                @pl.when((origin >= 0) & (origin < nz) & onward)
                def _():
                    chain(origin, way, k, h).wait_send()


def fused(n, inputs, value_grad, value_weight, counts, offsets):
    tok, width = inputs.shape
    half = value_grad.shape[1]
    wfeat, wcols = value_weight.shape
    nz = n // GROUP
    fq = wfeat // GROUP
    hr = width // n // 2
    bf, f32, dma = jnp.bfloat16, jnp.float32, pltpu.SemaphoreType.DMA
    normalizer = 1.0 / math.sqrt(counts.shape[1] * n)
    vmem = pl.BlockSpec(memory_space=pltpu.VMEM)
    smem = pl.BlockSpec(memory_space=pltpu.SMEM)
    hbm = pl.BlockSpec(memory_space=pltpu.HBM)
    return pl.pallas_call(
        functools.partial(kernel, n, normalizer),
        out_shape=(
            jax.ShapeDtypeStruct((tok, wfeat), bf),
            jax.ShapeDtypeStruct((2 * hr, half), f32),
        ),
        in_specs=[smem] * 2 + [hbm] * 3,
        out_specs=(vmem, vmem),
        scratch_shapes=[
            pltpu.VMEM((tok, width), bf),
            pltpu.VMEM((tok, half), bf),
            pltpu.VMEM((wcols, wfeat), bf),
            pltpu.VMEM((tok, half), bf),
            pltpu.VMEM((GROUP * tok, half), bf),
            pltpu.VMEM((GROUP * tok, half), bf),
            pltpu.VMEM((nz, GROUP * tok, hr), bf),
            pltpu.VMEM((n * wcols, fq), bf),
            pltpu.VMEM((nz, 2, hr, half), f32),
            pltpu.VMEM((nz, 2, hr, half), bf),
            pltpu.VMEM((2, nz, 2, hr, half), bf),
            pltpu.VMEM((hr, half), f32),
            pltpu.VMEM((hr, half), f32),
            pltpu.VMEM((GROUP, tok, fq), bf),
            pltpu.VMEM((GROUP, tok, fq), bf),
            dma((3,)),
            dma((GROUP,)), dma((GROUP,)),
            dma((GROUP + 1,)), dma((GROUP + 1,)),
            dma((GROUP,)), dma((GROUP,)),
            dma((nz, GROUP)), dma((nz, GROUP)),
            dma((2, nz, 2)), dma((nz, 2)),
            dma((nz, 2)), dma((2, nz, 2)),
            dma((GROUP,)), dma((GROUP,)),
            dma, dma,
        ],
        compiler_params=pltpu.CompilerParams(
            collective_id=0, has_side_effects=True, vmem_limit_bytes=VMEM_ROOM
        ),
    )(counts, offsets, inputs, value_grad, value_weight.T)


def solution(mesh):
    n, tp = mesh.shape["fsdp"], mesh.shape["tp"]

    def local(inputs, value_grad, value_weight, counts, offsets):
        hr = inputs.shape[1] // n // 2
        fits = tp == 2 and n % GROUP == 0 and n > GROUP and hr % 128 == 0
        fits = fits and value_weight.shape[1] % 16 == 0
        if fits:
            return fused(n, inputs, value_grad, value_weight, counts, offsets)
        return general(inputs, value_grad, value_weight, counts, offsets)

    in_specs = (P("fsdp", None), P("fsdp", "tp"), P("tp", "fsdp"), P("fsdp", None), P("fsdp", None))
    out_specs = (P("fsdp", "tp"), P("fsdp", "tp"))
    return jax.shard_map(local, mesh=mesh, in_specs=in_specs, out_specs=out_specs, check_vma=False)
```

time: 64.9 us -> 53.6 us (0.83)
  Pallas kernels: 56.5 us -> 46.1 us
  other arithmetic: 3.13 us -> 0 us
  local copies, waits for them, and re-layouts: 4.3 us -> 6.56 us
    pallas_call x1, Pallas kernels: 56.5 us -> 46.1 us  [fused(): pl.pallas_call(functools.partial(kernel, n, normalizer), out_shape=(jax.S...]
    unnamed x6 -> x12, local copies, waits for them, and re-layouts: 4.3 us -> 6.56 us
    convert_element_type x1 -> x0, other arithmetic: 1.05 us -> none  [scale_rows(): (value_grad.astype(jnp.float32) * row_factor[:, None]).astype(jnp.bfloat16)]
    reduce_sum x1 -> x0, other arithmetic: 0.74 us -> none  [scale_rows(): jnp.sum(jnp.where(inside, inverse_root, jnp.zeros_like(inverse_root)), ax...]
    lt x1 -> x0, other arithmetic: 0.68 us -> none  [scale_rows(): inside = (positions >= starts) & (positions < starts + lengths)]
    broadcast_in_dim x1 -> x0, other arithmetic: 0.66 us -> none  [scale_rows(): jnp.where(inside, inverse_root, jnp.zeros_like(inverse_root))]
where the time goes in v2:
time: 53.6 us; the launch traced here: 53.3 us
  Pallas kernels  46.1 us (86%)
  local copies, waits for them, and re-layouts  6.56 us (12%)
  between operations  0.65 us (1%)
    pallas_call x1, Pallas kernels, fused(): pl.pallas_call(functools.partial(kernel, n, normalizer), out_shape=(jax.S...  46.1 us
    unnamed x12, local copies, waits for them, and re-layouts  6.56 us

profile of v2, /device:TPU:0, one launch (start us, length us, event | category | flops | bytes accessed | tf_op | source)
XLA Modules:
  0.0 53.3 jit_solution(6982988732214145871)
XLA Ops:
  0.6 0.0 copy-start
  0.6 1.6 %copy-done = bf16[256,4096]{1,0:T(8,128)(2,1)S(1)} copy-done((bf16[256,4096]{1,0:T(8,128)(2,1)S(1)}, bf16[256,4096]{1,0:T(8,128)(2,1)}, u32[]{:S(2)}) %copy-start) | copy-done | bytes 2097176
  2.2 0.0 copy-start.1
  2.2 0.9 %copy-done.1 = bf16[256,512]{1,0:T(8,128)(2,1)S(1)} copy-done((bf16[256,512]{1,0:T(8,128)(2,1)S(1)}, bf16[256,512]{1,0:T(8,128)(2,1)}, u32[]{:S(2)}) %copy-start.1) | copy-done | bytes 262168
  3.2 0.0 copy-start.2
  3.2 0.9 %copy-done.2 = bf16[2048,64]{0,1:T(8,128)(2,1)S(1)} copy-done((bf16[2048,64]{0,1:T(8,128)(2,1)S(1)}, bf16[2048,64]{0,1:T(8,128)(2,1)}, u32[]{:S(2)}) %copy-start.2) | copy-done | bytes 262168
  4.1 0.0 copy-start.3
  4.1 0.7 %copy-done.3 = s32[1,4]{1,0:T(1,128)S(1)} copy-done((s32[1,4]{1,0:T(1,128)S(1)}, s32[1,4]{1,0:T(1,128)}, u32[]{:S(2)}) %copy-start.3) | copy-done | bytes 40
  4.8 0.0 copy-start.4
  4.8 0.7 %copy-done.4 = s32[1,4]{1,0:T(1,128)S(1)} copy-done((s32[1,4]{1,0:T(1,128)S(1)}, s32[1,4]{1,0:T(1,128)}, u32[]{:S(2)}) %copy-start.4) | copy-done | bytes 40
  5.4 46.1 %shard_map.68 = (bf16[256,2048]{1,0:T(8,128)(2,1)S(1)}, f32[256,512]{1,0:T(8,128)S(1)}) custom-call(s32[1,4]{1,0:T(1,128)S(1)} %copy-done.3, s32[1,4]{1,0:T(1,128)S(1)} %copy-done.4, bf16[256,4096]{1,0:T(8,128)(2,1)S(1)} %copy-done, bf16[256,512]{1,0:T(8,128)(2,1)S(1)} %copy-done.1, bf16[64,2048]{1,0:T(8,128)(2,1)S(1)} %bitcast.1), custom_call_target="tpu_custom_call" | custom-call | tf_op jit(solution)/shard_map/pallas_call | solution.py:338
  51.6 1.0 %copy.9 = bf16[256,2048]{1,0:T(8,128)(2,1)} copy(bf16[256,2048]{1,0:T(8,128)(2,1)S(1)} %get-tuple-element.4) | data formatting | bytes 2097152
  52.5 0.8 %copy.10 = f32[256,512]{1,0:T(8,128)} copy(f32[256,512]{1,0:T(8,128)S(1)} %get-tuple-element.5) | data formatting | bytes 1048576
Async XLA Ops:
  0.6 1.6 %copy-start = (bf16[256,4096]{1,0:T(8,128)(2,1)S(1)}, bf16[256,4096]{1,0:T(8,128)(2,1)}, u32[]{:S(2)}) copy-start(bf16[256,4096]{1,0:T(8,128)(2,1)} %x_hbm.1) | copy-start | bytes 6291460
  2.2 0.9 %copy-start.1 = (bf16[256,512]{1,0:T(8,128)(2,1)S(1)}, bf16[256,512]{1,0:T(8,128)(2,1)}, u32[]{:S(2)}) copy-start(bf16[256,512]{1,0:T(8,128)(2,1)} %g_hbm.1) | copy-start | bytes 786436
  3.2 0.9 %copy-start.2 = (bf16[2048,64]{0,1:T(8,128)(2,1)S(1)}, bf16[2048,64]{0,1:T(8,128)(2,1)}, u32[]{:S(2)}) copy-start(bf16[2048,64]{0,1:T(8,128)(2,1)} %param.7) | copy-start | bytes 786436
  4.1 0.7 %copy-start.3 = (s32[1,4]{1,0:T(1,128)S(1)}, s32[1,4]{1,0:T(1,128)}, u32[]{:S(2)}) copy-start(s32[1,4]{1,0:T(1,128)} %counts_ref.1) | copy-start | bytes 52
  4.8 0.7 %copy-start.4 = (s32[1,4]{1,0:T(1,128)S(1)}, s32[1,4]{1,0:T(1,128)}, u32[]{:S(2)}) copy-start(s32[1,4]{1,0:T(1,128)} %offsets_ref.1) | copy-start | bytes 52

commit v3 on v2

--- a/solution.py
+++ b/solution.py
@@ -10,7 +10,7 @@
 
 MESH = pl.DeviceIdType.MESH
 GROUP = 4
-VMEM_ROOM = 48 * 2**20
+VMEM_ROOM = 58 * 2**20
 
 
 def scale_rows(value_grad, counts, offsets):

time: 53.6 us -> 51.2 us (0.955)
  local copies, waits for them, and re-layouts: 6.56 us -> 3.16 us
  Pallas kernels: 46.1 us -> 47.2 us
    unnamed x12 -> x4, local copies, waits for them, and re-layouts: 6.56 us -> 3.16 us
    pallas_call x1, Pallas kernels: 46.1 us -> 47.2 us  [fused(): pl.pallas_call(functools.partial(kernel, n, normalizer), out_shape=(jax.S...]
where the time goes in v3:
time: 51.2 us; the launch traced here: 51 us
  Pallas kernels  47.2 us (92%)
  local copies, waits for them, and re-layouts  3.16 us (6%)
  between operations  0.65 us (1%)
    pallas_call x1, Pallas kernels, fused(): pl.pallas_call(functools.partial(kernel, n, normalizer), out_shape=(jax.S...  47.2 us
    unnamed x4, local copies, waits for them, and re-layouts  3.16 us

profile of v3, /device:TPU:0, one launch (start us, length us, event | category | flops | bytes accessed | tf_op | source)
XLA Modules:
  0.0 51.0 jit_solution(5397893373069408621)
XLA Ops:
  0.6 47.2 %shard_map.68 = (bf16[256,2048]{1,0:T(8,128)(2,1)}, f32[256,512]{1,0:T(8,128)}) custom-call(s32[1,4]{1,0:T(1,128)} %counts_ref.1, s32[1,4]{1,0:T(1,128)} %offsets_ref.1, bf16[256,4096]{1,0:T(8,128)(2,1)} %x_hbm.1, bf16[256,512]{1,0:T(8,128)(2,1)} %g_hbm.1, bf16[64,2048]{1,0:T(8,128)(2,1)} %bitcast.1), custom_call_target="tpu_custom_call" | custom-call | tf_op jit(solution)/shard_map/pallas_call | solution.py:338
  47.9 0.0 copy-start
  47.9 2.4 %copy.9 = bf16[256,2048]{1,0:T(8,128)(2,1)} copy(bf16[256,2048]{1,0:T(8,128)(2,1)} %get-tuple-element.4) | data formatting | bytes 2097152
  50.2 0.0 copy-done
  50.2 0.8 %copy.10 = f32[256,512]{1,0:T(8,128)} copy(f32[256,512]{1,0:T(8,128)S(1)} %copy-done) | data formatting | bytes 1048576
Async XLA Ops:
  47.9 2.4 %copy-start = (f32[256,512]{1,0:T(8,128)S(1)}, f32[256,512]{1,0:T(8,128)}, u32[]{:S(2)}) copy-start(f32[256,512]{1,0:T(8,128)} %get-tuple-element.5) | copy-start | bytes 1572868
